TPU v7x, 32 devices: a whole 2x2x4 slice. The times are simulated.
32 devices in a mesh: replica: 8 (over z, core), fsdp: 4 (over y, x).
Axes of the slice: x: 2, y: 2, z: 4, core: 2. Of those that a mesh axis runs over, the one named last changes fastest.
Arguments:
- acts: bfloat16 [1, 4096, 8192], P(None, ('replica', 'fsdp')), may hold values from -6 to 6
- key_cot: bfloat16 [1, 4096, 512], P(None, ('replica', 'fsdp')), may hold values from -0.29882812 to 0.29882812
- params: float32 [8192, 512], P('fsdp'), may hold values from -4 to 4
- moment_one: float32 [8192, 512], P('fsdp'), may hold values from -1.8 to 1.8
- moment_two: float32 [8192, 512], P('fsdp'), may hold values from 0.05 to 2
- outer_mom: float32 [8192, 512], P(('fsdp', 'replica')), may hold values from -1.8 to 1.8
Outputs:
- new_params: float32 [8192, 512], P(('fsdp', 'replica'))
- new_mom: float32 [8192, 512], P(('fsdp', 'replica'))
All inputs are finite; a program needn't handle non-finite values.
Results may differ from a plain program's by a relative error of at most 0.0007.
Values may be sent and summed in bfloat16 or wider, within the bound.
A program may use at most 64 MiB of HBM per device.

v0:
```python
import functools

import jax
import jax.numpy as jnp
from jax import lax
from jax.experimental import pallas as pl
from jax.experimental.pallas import tpu as pltpu
from jax.sharding import PartitionSpec as P

beta_one = 0.9
beta_two = 0.95
epsilon = 1e-08
inner_rate = 0.3
decay_rate = 0.1
outer_rate = 0.7
momentum = 0.9

MESH = pl.DeviceIdType.MESH
UNIT = 128
WINDOW = 4

def adamw_direction(first, second, gradient):
    first = beta_one * first + (1.0 - beta_one) * gradient
    second = beta_two * second + (1.0 - beta_two) * gradient * gradient
    return first / (jnp.sqrt(second) + epsilon)

def kernel(
    n_rep, splits,
    acts_ref, cot_ref, params_ref, first_ref, second_ref, outer_ref, new_params_ref, new_mom_ref,
    acts_buf, cot_buf, first_buf, second_buf, pair_out, pair_in, far_out, far_in, own_sum, anchor_buf, outer_buf,
    acts_send, acts_recv, cot_send, cot_recv, pair_send, pair_recv, far_send, far_recv, state_sem, local_sem,
):
    rep = lax.axis_index("replica")
    shard = lax.axis_index("fsdp")
    line, core = lax.div(rep, 2), lax.rem(rep, 2)
    row_at, col_at = lax.div(shard, 2), lax.rem(shard, 2)
    rows = first_ref.shape[0]
    block = rows // n_rep
    half = cot_ref.shape[0] // 2
    tokens = acts_buf.shape[0] * acts_buf.shape[1]
    width = cot_buf.shape[2]
    partner = line * 2 + (1 - core)
    shards = (shard, row_at * 2 + (1 - col_at), (1 - row_at) * 2 + col_at, (1 - row_at) * 2 + (1 - col_at))
    lines = (line, line + 1 - 2 * lax.rem(line, 2), lax.rem(line + 2, 4), 3 - line)
    outer = 1 - lax.rem(lax.div(line, 2) + lax.rem(line, 2), 2)
    is_outer = outer == 1
    n_line = len(lines)

    units = []
    for k in range(n_line):
        other = lines[n_line - 1 - k]
        size = block // splits[k]
        for h, owner in ((0, 1 - core), (1, core)):
            for part in range(splits[k]):
                units.append((k, part * size, size, h, other * 2 + owner))

    def span(start, size):
        return pl.ds(pl.multiple_of(start, size), size)

    def remote(source, target, send, recv, device):
        return pltpu.make_async_remote_copy(
            src_ref=source, dst_ref=target, send_sem=send, recv_sem=recv, device_id=device, device_id_type=MESH
        )

    local = [
        pltpu.make_async_copy(cot_ref, cot_buf.at[0], local_sem.at[0]),
        pltpu.make_async_copy(acts_ref.at[:, span(shard * rows, rows)], acts_buf.at[0], local_sem.at[1]),
    ]
    state = []
    for i, (k, start, size, h, j) in enumerate(units):
        at = span(j * block + start, size)
        state.append((
            pltpu.make_async_copy(first_ref.at[at], first_buf.at[at], state_sem.at[i, 0]),
            pltpu.make_async_copy(second_ref.at[at], second_buf.at[at], state_sem.at[i, 1]),
        ))
    barrier = pltpu.get_barrier_semaphore()
    peers = [(rep, shards[d]) for d in range(1, 4)] + [(partner, shard)]
    peers += [(lines[o] * 2 + core, shard) for o in (1, 2)]
    for peer in peers:
        pl.semaphore_signal(barrier, inc=1, device_id=peer, device_id_type=MESH)

    @pl.when(jnp.logical_not(is_outer))
    def _():
        pl.semaphore_signal(barrier, inc=1, device_id=(lines[3] * 2 + core, shard), device_id_type=MESH)

    for copy in local:
        copy.start()
    pl.semaphore_wait(barrier, len(peers) + 1 - outer)

    sends = []
    cots = []
    for d in (1, 2):
        copy = remote(cot_ref, cot_buf.at[d], cot_send.at[d], cot_recv.at[d], (rep, shards[d]))
        copy.start()
        cots.append(copy)
    moves = []

    def issue(i):
        k, start, size, h, j = units[i]
        group = []
        for d in (3, 1, 2):
            copy = remote(
                acts_ref.at[:, span(shards[d] * rows + j * block + start, size)],
                acts_buf.at[d, :, span(j * block + start, size)],
                acts_send.at[i, d], acts_recv.at[i, d], (rep, shards[d]),
            )
            copy.start()
            group.append(copy)
        moves.append(group)
        for copy in state[i]:
            copy.start()

    for i in range(2):
        issue(i)
    for d, via in ((1, 2), (2, 1)):
        cots[d - 1].wait_recv()
        piece = pl.ds((d - 1) * half, half)
        copy = remote(
            cot_buf.at[d, piece], cot_buf.at[3, piece], cot_send.at[d + 2], cot_recv.at[d + 2], (rep, shards[via])
        )
        copy.start()
        cots.append(copy)
    for i in range(2, WINDOW):
        issue(i)
    finals = [
        pltpu.make_async_copy(params_ref.at[span(rep * block, block)], anchor_buf, local_sem.at[2]),
        pltpu.make_async_copy(outer_ref, outer_buf, local_sem.at[3]),
    ]
    for copy in finals:
        copy.start()
    for copy in local:
        copy.wait()
    for copy in cots[2:]:
        copy.wait_recv()

    far_sends = []
    pairings = {}
    for i, (k, start, size, h, j) in enumerate(units):
        last = k == n_line - 1
        for copy in moves[i]:
            copy.wait_recv()
        if i + WINDOW < len(units):
            issue(i + WINDOW)
        for copy in state[i]:
            copy.wait()
        at = span(j * block + start, size)
        here = pl.ds(start, size)
        gradient = lax.dot_general(
            acts_buf[:, :, at].reshape(tokens, size), cot_buf[...].reshape(tokens, width),
            (((0,), (0,)), ((), ())), preferred_element_type=jnp.float32,
        )
        value = adamw_direction(first_buf[at, :], second_buf[at, :], gradient)
        sem = (k, start // size)
        if h == 0:
            pair_out[k, here, :] = value
            pairing = remote(
                pair_out.at[k, here], pair_in.at[k, here], pair_send.at[sem], pair_recv.at[sem], (partner, shard)
            )
            pairing.start()
            pairings[sem] = pairing
            sends.append(pairing)
            continue
        pairings[sem].wait_recv()
        value = value + pair_in[k, here, :]
        if last:
            own_sum[here, :] = value
            continue
        if k == 0:
            slot = outer * 3
            device = ((outer * lines[1] + (1 - outer) * lines[3]) * 2 + core, shard)
        else:
            slot = k
            device = (j, shard)
        if k == 1:
            arrival = remote(
                far_out.at[k, here], far_in.at[3, here],
                far_send.at[3, start // size], far_recv.at[3, start // size], device,
            )

            @pl.when(is_outer)
            def _(value=value, k=k, here=here):
                far_out[k, here, :] = value.astype(jnp.bfloat16)

            @pl.when(jnp.logical_not(is_outer))
            def _(value=value, k=k, here=here, arrival=arrival):
                arrival.wait_recv()
                far_out[k, here, :] = (value + far_in[3, here, :].astype(jnp.float32)).astype(jnp.bfloat16)
        else:
            far_out[k, here, :] = value.astype(jnp.bfloat16)
        copy = remote(
            far_out.at[k, here], far_in.at[slot, here],
            far_send.at[sem], far_recv.at[slot, start // size], device,
        )
        copy.start()
        far_sends.append((k, start, size, copy))

    for k, start, size, copy in far_sends:
        if k > 0:
            copy.wait_recv()
        else:
            arrival = remote(
                far_out.at[0, pl.ds(start, size)], far_in.at[0, pl.ds(start, size)],
                far_send.at[0, start // size], far_recv.at[0, start // size], (rep, shard),
            )

            @pl.when(jnp.logical_not(is_outer))
            def _(arrival=arrival):
                arrival.wait_recv()

    @pl.when(jnp.logical_not(is_outer))
    def _():
        own_sum[...] = own_sum[...] + far_in[0].astype(jnp.float32)

    for copy in finals:
        copy.wait()
    anchor = anchor_buf[...]
    total = own_sum[...] + (far_in[1].astype(jnp.float32) + far_in[2].astype(jnp.float32))
    drift_mean = inner_rate * (total / n_rep + decay_rate * anchor)
    new_mom = momentum * outer_buf[...] + drift_mean
    new_params_ref[...] = anchor - outer_rate * (drift_mean + momentum * new_mom)
    new_mom_ref[...] = new_mom

    for copy in cots + sends + [entry[3] for entry in far_sends]:
        copy.wait_send()
    for group in moves:
        for copy in group:
            copy.wait_send()

def fused_round(acts, cot, params, first, second, outer, n_rep, n_fsdp):
    tokens, width = cot.shape
    rows = first.shape[0]
    block = rows // n_rep
    n_line = n_rep // 2
    splits = (block // UNIT,) * n_line
    units = 2 * sum(splits)
    parts = max(splits)
    return pl.pallas_call(
        functools.partial(kernel, n_rep, splits),
        out_shape=(pltpu.VMEM((block, width), jnp.float32),) * 2,
        in_specs=[pl.BlockSpec(memory_space=pltpu.HBM)] * 6,
        out_specs=(pl.BlockSpec(memory_space=pltpu.VMEM),) * 2,
        scratch_shapes=[
            pltpu.VMEM((n_fsdp, tokens, rows), jnp.bfloat16),
            pltpu.VMEM((n_fsdp, tokens, width), jnp.bfloat16),
            pltpu.VMEM((rows, width), jnp.float32),
            pltpu.VMEM((rows, width), jnp.float32),
            pltpu.VMEM((n_line, block, width), jnp.float32),
            pltpu.VMEM((n_line, block, width), jnp.float32),
            pltpu.VMEM((n_line, block, width), jnp.bfloat16),
            pltpu.VMEM((n_line, block, width), jnp.bfloat16),
            pltpu.VMEM((block, width), jnp.float32),
            pltpu.VMEM((block, width), jnp.float32),
            pltpu.VMEM((block, width), jnp.float32),
            pltpu.SemaphoreType.DMA((units, n_fsdp)),
            pltpu.SemaphoreType.DMA((units, n_fsdp)),
            pltpu.SemaphoreType.DMA((5,)),
            pltpu.SemaphoreType.DMA((5,)),
            pltpu.SemaphoreType.DMA((n_line, parts)),
            pltpu.SemaphoreType.DMA((n_line, parts)),
            pltpu.SemaphoreType.DMA((n_line, parts)),
            pltpu.SemaphoreType.DMA((n_line, parts)),
            pltpu.SemaphoreType.DMA((units, 2)),
            pltpu.SemaphoreType.DMA((4,)),
        ],
        compiler_params=pltpu.CompilerParams(collective_id=0, has_side_effects=True),
    )(acts, cot, params, first, second, outer)

def plain_sum(acts, cot, first, second):
    inputs = lax.all_to_all(acts, "fsdp", split_axis=1, concat_axis=0, tiled=True)
    cots = lax.all_gather(cot, "fsdp", axis=0, tiled=True)
    gradient = lax.dot_general(
        inputs, cots, (((0,), (0,)), ((), ())), preferred_element_type=jnp.float32
    )
    return lax.psum_scatter(
        adamw_direction(first, second, gradient), "replica", scatter_dimension=0, tiled=True
    )

def per_device(n_rep, n_fsdp, acts, key_cot, params, moment_one, moment_two, outer_mom):
    block = params.shape[0] // n_rep
    acts, key_cot = acts[0], key_cot[0]
    if block % UNIT == 0 and n_rep == 8 and n_fsdp == 4:
        return fused_round(acts, key_cot, params, moment_one, moment_two, outer_mom, n_rep, n_fsdp)
    total = plain_sum(acts, key_cot, moment_one, moment_two)
    anchor = lax.dynamic_slice_in_dim(params, lax.axis_index("replica") * block, block, 0)
    drift_mean = inner_rate * (total / n_rep + decay_rate * anchor)
    new_mom = momentum * outer_mom + drift_mean
    new_params = anchor - outer_rate * (drift_mean + momentum * new_mom)
    return (new_params, new_mom)

def solution(mesh):
    return jax.shard_map(
        functools.partial(per_device, mesh.shape["replica"], mesh.shape["fsdp"]),
        mesh=mesh,
        in_specs=(
            P(None, ("replica", "fsdp"), None),
            P(None, ("replica", "fsdp"), None),
            P("fsdp", None),
            P("fsdp", None),
            P("fsdp", None),
            P(("fsdp", "replica"), None),
        ),
        out_specs=(P(("fsdp", "replica"), None), P(("fsdp", "replica"), None)),
        check_vma=False,
    )
```

profile of v0, /device:TPU:0, one launch (start us, length us, event | category | flops | bytes accessed | tf_op | source)
XLA Modules:
  0.0 44.5 jit_solution(5848822042365047959)
XLA Ops:
  0.6 42.2 %shard_map.77 = (f32[256,512]{1,0:T(8,128)S(1)}, f32[256,512]{1,0:T(8,128)S(1)}) custom-call(bf16[128,8192]{1,0:T(8,128)(2,1)} %bitcast.2, bf16[128,512]{1,0:T(8,128)(2,1)} %bitcast.3, f32[2048,512]{1,0:T(8,128)} %params_ref.1, f32[2048,512]{1,0:T(8,128)} %first_ref.1, f32[2048,512]{1,0:T(8,128)} %second_ref.1, f32[256,512]{1,0:T(8,128)} %outer_ref.1), custom_call_target="tpu_custom_call" | custom-call | tf_op jit(solution)/shard_map/pallas_call | solution.py:237
  42.9 0.8 %copy.10 = f32[256,512]{1,0:T(8,128)} copy(f32[256,512]{1,0:T(8,128)S(1)} %get-tuple-element.2) | data formatting | bytes 1048576
  43.7 0.8 %copy.11 = f32[256,512]{1,0:T(8,128)} copy(f32[256,512]{1,0:T(8,128)S(1)} %get-tuple-element.3) | data formatting | bytes 1048576
where the time goes:
time: 44.6 us; the launch traced here: 44.5 us
  Pallas kernels  42.2 us (95%)
  local copies, waits for them, and re-layouts  1.59 us (4%)
  between operations  0.64 us (1%)
    pallas_call x1, Pallas kernels, fused_round(): pl.pallas_call(functools.partial(kernel, n_rep, splits), out_shape=(pltpu...  42.2 us
    unnamed x2, local copies, waits for them, and re-layouts  1.59 us

commit v1 on v0

v1 whole, which is shorter than its diff:
```python
import functools

import jax
import jax.numpy as jnp
from jax import lax
from jax.experimental import pallas as pl
from jax.experimental.pallas import tpu as pltpu
from jax.sharding import PartitionSpec as P

beta_one = 0.9
beta_two = 0.95
epsilon = 1e-08
inner_rate = 0.3
decay_rate = 0.1
outer_rate = 0.7
momentum = 0.9

MESH = pl.DeviceIdType.MESH
OUTER_PLAN = (
    (3, 0, 1, 3, None), (2, 0, 2, 2, None), (3, 1, 1, 3, None), (2, 1, 1, 2, None),
    (1, 0, 1, 0, None), (1, 1, 1, 0, None), (0, 0, None, None, None), (0, 1, None, None, None),
)
INNER_PLAN = (
    (3, 0, 3, 1, None), (1, 0, 1, 0, None), (2, 0, 2, 1, (3, 0)), (1, 1, 1, 0, None),
    (2, 1, 2, 1, (3, 1)), (3, 1, 3, 1, (2, 1)), (0, 0, None, None, None), (0, 1, None, None, None),
)
UNIT = 128
WINDOW = 5
EARLY = 1
AFTER = 4

def adamw_direction(first, second, gradient):
    first = beta_one * first + (1.0 - beta_one) * gradient
    second = beta_two * second + (1.0 - beta_two) * gradient * gradient
    return first / (jnp.sqrt(second) + epsilon)

def kernel(
    n_rep,
    acts_ref, cot_ref, params_ref, first_ref, second_ref, outer_ref, new_params_ref, new_mom_ref,
    acts_buf, cot_buf, first_buf, second_buf, pair_out, pair_in, far_out, far_in, stash, anchor_buf, outer_buf,
    acts_recv, cot_recv, pair_recv, far_recv, send_sem, local_sem,
):
    rep = lax.axis_index("replica")
    shard = lax.axis_index("fsdp")
    line, core = lax.div(rep, 2), lax.rem(rep, 2)
    row_at, col_at = lax.div(shard, 2), lax.rem(shard, 2)
    rows = first_ref.shape[0]
    block = rows // n_rep
    size = block // 2
    half = cot_ref.shape[0] // 2
    tokens = acts_buf.shape[0] * acts_buf.shape[1]
    width = cot_buf.shape[2]
    partner = line * 2 + (1 - core)
    shards = (shard, row_at * 2 + (1 - col_at), (1 - row_at) * 2 + col_at, (1 - row_at) * 2 + (1 - col_at))
    lines = (line, line + 1 - 2 * lax.rem(line, 2), lax.rem(line + 2, 4), 3 - line)
    outer = 1 - lax.rem(lax.div(line, 2) + lax.rem(line, 2), 2)
    is_outer = outer == 1
    is_inner = jnp.logical_not(is_outer)

    def span(start, length):
        return pl.ds(pl.multiple_of(start, length), length)

    def remote(source, target, send, recv, device):
        return pltpu.make_async_remote_copy(
            src_ref=source, dst_ref=target, send_sem=send, recv_sem=recv, device_id=device, device_id_type=MESH
        )

    def pick(at_outer, at_inner):
        return outer * at_outer + (1 - outer) * at_inner

    units = []
    for step, (at_outer, at_inner) in enumerate(zip(OUTER_PLAN, INNER_PLAN)):
        other = pick(lines[at_outer[0]], lines[at_inner[0]])
        start = pick(at_outer[1], at_inner[1]) * size
        for h, owner in ((0, 1 - core), (1, core)):
            units.append((step, h, (other * 2 + owner) * block + start))

    barrier = pltpu.get_barrier_semaphore()
    peers = [(rep, shards[d]) for d in (3, 1, 2)] + [(partner, shard)]
    peers += [(lines[o] * 2 + core, shard) for o in (1, 2)]
    for peer in peers:
        pl.semaphore_signal(barrier, inc=1, device_id=peer, device_id_type=MESH)

    @pl.when(is_inner)
    def _():
        pl.semaphore_signal(barrier, inc=1, device_id=(lines[3] * 2 + core, shard), device_id_type=MESH)

    local = [
        pltpu.make_async_copy(cot_ref, cot_buf.at[0], local_sem.at[0]),
        pltpu.make_async_copy(acts_ref.at[:, span(shard * rows, rows)], acts_buf.at[0], local_sem.at[1]),
        pltpu.make_async_copy(first_ref, first_buf, local_sem.at[2]),
        pltpu.make_async_copy(second_ref, second_buf, local_sem.at[3]),
    ]
    finals = [
        pltpu.make_async_copy(params_ref.at[span(rep * block, block)], anchor_buf, local_sem.at[4]),
        pltpu.make_async_copy(outer_ref, outer_buf, local_sem.at[5]),
    ]
    for copy in local[:2]:
        copy.start()
    pl.semaphore_wait(barrier, len(peers) + 1 - outer)

    pieces = (pl.ds(0, half), pl.ds(half, half))
    direct = {}
    for turn in range(2):
        for d in (1, 2):
            piece = (d - 1 + turn) % 2
            direct[d, piece] = remote(
                cot_ref.at[pieces[piece]], cot_buf.at[d, pieces[piece]],
                send_sem.at[0], cot_recv.at[d - 1, piece], (rep, shards[d]),
            )
            direct[d, piece].start()

    for copy in local[2:] + finals:
        copy.start()

    def issue(i):
        at = units[i][2]
        for d in (3, 1, 2):
            remote(
                acts_ref.at[:, span(shards[d] * rows + at, size)], acts_buf.at[d, :, span(at, size)],
                send_sem.at[1], acts_recv.at[i], (rep, shards[d]),
            ).start()

    for i in range(EARLY):
        issue(i)
    relays = []
    for d, via in ((1, 2), (2, 1)):
        piece = d - 1
        direct[d, piece].wait_recv()
        relay = remote(
            cot_buf.at[d, pieces[piece]], cot_buf.at[3, pieces[piece]],
            send_sem.at[0], cot_recv.at[2, piece], (rep, shards[via]),
        )
        relay.start()
        relays.append(relay)
    for i in range(EARLY, AFTER):
        issue(i)
    for copy in local:
        copy.wait()
    for d in (1, 2):
        direct[d, 2 - d].wait_recv()
    for copy in relays:
        copy.wait_recv()
    for i in range(AFTER, WINDOW):
        issue(i)

    def arrival(slot, part):
        piece = far_in.at[slot, part]
        return remote(piece, piece, send_sem.at[3], far_recv.at[slot, part], (partner, shard))

    def forward(step):
        at_outer, at_inner = OUTER_PLAN[step], INNER_PLAN[step]
        slot, part = pick(at_outer[3], at_inner[3]), pick(at_outer[1], at_inner[1])
        line_to = pick(lines[at_outer[2]], lines[at_inner[2]])
        remote(
            far_out.at[step], far_in.at[slot, part], send_sem.at[3], far_recv.at[slot, part],
            (line_to * 2 + core, shard),
        ).start()

    def combine(step):
        slot, part = INNER_PLAN[step][4]

        @pl.when(is_inner)
        def _():
            arrival(slot, part).wait_recv()
            far_out[step] = (stash[step] + far_in[slot, part].astype(jnp.float32)).astype(jnp.bfloat16)
            forward(step)

    held = []
    for i, (step, h, at) in enumerate(units):
        rows_at = span(at, size)
        arrived = acts_buf.at[1:, :, rows_at]
        remote(arrived, arrived, send_sem.at[1], acts_recv.at[i], (rep, shards[1])).wait_recv()
        if h == 0 and i + WINDOW < len(units):
            issue(i + WINDOW)
        gradient = lax.dot_general(
            acts_buf[:, :, rows_at].reshape(tokens, size), cot_buf[...].reshape(tokens, width),
            (((0,), (0,)), ((), ())), preferred_element_type=jnp.float32,
        )
        value = adamw_direction(first_buf[rows_at, :], second_buf[rows_at, :], gradient)
        pairing = remote(
            pair_out.at[step], pair_in.at[step], send_sem.at[2], pair_recv.at[step], (partner, shard)
        )
        if h == 0:
            pair_out[step] = value
            pairing.start()
            while held:
                combine(held.pop())
            continue
        pairing.wait_recv()
        value = value + pair_in[step]
        part = OUTER_PLAN[step][1]
        if OUTER_PLAN[step][2] is None:
            stash[step] = value
        elif INNER_PLAN[step][4] is None:
            far_out[step] = value.astype(jnp.bfloat16)
            forward(step)
        else:
            held.append(step)

            @pl.when(is_inner)
            def _(value=value, step=step):
                stash[step] = value

            @pl.when(is_outer)
            def _(value=value, step=step):
                far_out[step] = value.astype(jnp.bfloat16)
                forward(step)

        if i + WINDOW < len(units):
            issue(i + WINDOW)
        if OUTER_PLAN[step][2] is not None:
            continue
        if part == 0:
            for copy in finals:
                copy.wait()

            @pl.when(is_inner)
            def _(value=value, step=step):
                arrival(2, 0).wait_recv()
                stash[step] = value + far_in[2, 0].astype(jnp.float32)

        arrival(0, part).wait_recv()
        arrival(1, part).wait_recv()
        here = pl.ds(part * size, size)
        total = stash[step] + (far_in[0, part].astype(jnp.float32) + far_in[1, part].astype(jnp.float32))
        anchor = anchor_buf[here, :]
        drift_mean = inner_rate * (total / n_rep + decay_rate * anchor)
        new_mom = momentum * outer_buf[here, :] + drift_mean
        new_params_ref[here, :] = anchor - outer_rate * (drift_mean + momentum * new_mom)
        new_mom_ref[here, :] = new_mom

    for j, sent in enumerate((cot_buf.at[1:], acts_buf.at[1:], pair_out, far_out)):
        remote(sent, sent, send_sem.at[j], send_sem.at[j], (partner, shard)).wait_send()

def fused_round(acts, cot, params, first, second, outer, n_rep, n_fsdp):
    tokens, width = cot.shape
    rows = first.shape[0]
    block = rows // n_rep
    size = block // 2
    steps = len(OUTER_PLAN)
    return pl.pallas_call(
        functools.partial(kernel, n_rep),
        out_shape=(pltpu.VMEM((block, width), jnp.float32),) * 2,
        in_specs=[pl.BlockSpec(memory_space=pltpu.HBM)] * 6,
        out_specs=(pl.BlockSpec(memory_space=pltpu.VMEM),) * 2,
        scratch_shapes=[
            pltpu.VMEM((n_fsdp, tokens, rows), jnp.bfloat16),
            pltpu.VMEM((n_fsdp, tokens, width), jnp.bfloat16),
            pltpu.VMEM((rows, width), jnp.float32),
            pltpu.VMEM((rows, width), jnp.float32),
            pltpu.VMEM((steps, size, width), jnp.float32),
            pltpu.VMEM((steps, size, width), jnp.float32),
            pltpu.VMEM((steps - 2, size, width), jnp.bfloat16),
            pltpu.VMEM((4, 2, size, width), jnp.bfloat16),
            pltpu.VMEM((steps, size, width), jnp.float32),
            pltpu.VMEM((block, width), jnp.float32),
            pltpu.VMEM((block, width), jnp.float32),
            pltpu.SemaphoreType.DMA((2 * steps,)),
            pltpu.SemaphoreType.DMA((3, 2)),
            pltpu.SemaphoreType.DMA((steps,)),
            pltpu.SemaphoreType.DMA((4, 2)),
            pltpu.SemaphoreType.DMA((4,)),
            pltpu.SemaphoreType.DMA((6,)),
        ],
        compiler_params=pltpu.CompilerParams(collective_id=0, has_side_effects=True),
    )(acts, cot, params, first, second, outer)

def plain_sum(acts, cot, first, second):
    inputs = lax.all_to_all(acts, "fsdp", split_axis=1, concat_axis=0, tiled=True)
    cots = lax.all_gather(cot, "fsdp", axis=0, tiled=True)
    gradient = lax.dot_general(
        inputs, cots, (((0,), (0,)), ((), ())), preferred_element_type=jnp.float32
    )
    return lax.psum_scatter(
        adamw_direction(first, second, gradient), "replica", scatter_dimension=0, tiled=True
    )

def per_device(n_rep, n_fsdp, acts, key_cot, params, moment_one, moment_two, outer_mom):
    block = params.shape[0] // n_rep
    acts, key_cot = acts[0], key_cot[0]
    if block % (2 * UNIT) == 0 and n_rep == 8 and n_fsdp == 4:
        return fused_round(acts, key_cot, params, moment_one, moment_two, outer_mom, n_rep, n_fsdp)
    total = plain_sum(acts, key_cot, moment_one, moment_two)
    anchor = lax.dynamic_slice_in_dim(params, lax.axis_index("replica") * block, block, 0)
    drift_mean = inner_rate * (total / n_rep + decay_rate * anchor)
    new_mom = momentum * outer_mom + drift_mean
    new_params = anchor - outer_rate * (drift_mean + momentum * new_mom)
    return (new_params, new_mom)

def solution(mesh):
    return jax.shard_map(
        functools.partial(per_device, mesh.shape["replica"], mesh.shape["fsdp"]),
        mesh=mesh,
        in_specs=(
            P(None, ("replica", "fsdp"), None),
            P(None, ("replica", "fsdp"), None),
            P("fsdp", None),
            P("fsdp", None),
            P("fsdp", None),
            P(("fsdp", "replica"), None),
        ),
        out_specs=(P(("fsdp", "replica"), None), P(("fsdp", "replica"), None)),
        check_vma=False,
    )
```

time: 44.6 us -> 37.2 us (0.83)
  Pallas kernels: 42.2 us -> 34.8 us
    pallas_call x1, Pallas kernels: 42.2 us -> 34.8 us  [fused_round(): pl.pallas_call(functools.partial(kernel, n_rep), out_shape=(pltpu.VMEM((b...]
where the time goes in v1:
time: 37.2 us; the launch traced here: 37 us
  Pallas kernels  34.8 us (94%)
  local copies, waits for them, and re-layouts  1.59 us (4%)
  between operations  0.64 us (2%)
    pallas_call x1, Pallas kernels, fused_round(): pl.pallas_call(functools.partial(kernel, n_rep), out_shape=(pltpu.VMEM((b...  34.8 us
    unnamed x2, local copies, waits for them, and re-layouts  1.59 us

profile of v1, /device:TPU:0, one launch (start us, length us, event | category | flops | bytes accessed | tf_op | source)
XLA Modules:
  0.0 37.0 jit_solution(17852982057664878930)
XLA Ops:
  0.6 34.8 %shard_map.77 = (f32[256,512]{1,0:T(8,128)S(1)}, f32[256,512]{1,0:T(8,128)S(1)}) custom-call(bf16[128,8192]{1,0:T(8,128)(2,1)} %bitcast.2, bf16[128,512]{1,0:T(8,128)(2,1)} %bitcast.3, f32[2048,512]{1,0:T(8,128)} %params_ref.1, f32[2048,512]{1,0:T(8,128)} %first_ref.1, f32[2048,512]{1,0:T(8,128)} %second_ref.1, f32[256,512]{1,0:T(8,128)} %outer_ref.1), custom_call_target="tpu_custom_call" | custom-call | tf_op jit(solution)/shard_map/pallas_call | solution.py:242
  35.4 0.8 %copy.10 = f32[256,512]{1,0:T(8,128)} copy(f32[256,512]{1,0:T(8,128)S(1)} %get-tuple-element.2) | data formatting | bytes 1048576
  36.2 0.8 %copy.11 = f32[256,512]{1,0:T(8,128)} copy(f32[256,512]{1,0:T(8,128)S(1)} %get-tuple-element.3) | data formatting | bytes 1048576

commit v2 on v1

--- a/solution.py
+++ b/solution.py
@@ -27,6 +27,7 @@
 UNIT = 128
 WINDOW = 5
 EARLY = 1
+PIECES = 2
 AFTER = 4
 
 def adamw_direction(first, second, gradient):
@@ -233,13 +234,24 @@
     for j, sent in enumerate((cot_buf.at[1:], acts_buf.at[1:], pair_out, far_out)):
         remote(sent, sent, send_sem.at[j], send_sem.at[j], (partner, shard)).wait_send()
 
+def write_out(params_ref, mom_ref, out_params_ref, out_mom_ref, sem):
+    rows = params_ref.shape[0] // PIECES
+    copies = []
+    for j, (source, target) in enumerate(((params_ref, out_params_ref), (mom_ref, out_mom_ref))):
+        for p in range(PIECES):
+            piece = pl.ds(p * rows, rows)
+            copies.append(pltpu.make_async_copy(source.at[piece], target.at[piece], sem.at[j, p]))
+            copies[-1].start()
+    for copy in copies:
+        copy.wait()
+
 def fused_round(acts, cot, params, first, second, outer, n_rep, n_fsdp):
     tokens, width = cot.shape
     rows = first.shape[0]
     block = rows // n_rep
     size = block // 2
     steps = len(OUTER_PLAN)
-    return pl.pallas_call(
+    results = pl.pallas_call(
         functools.partial(kernel, n_rep),
         out_shape=(pltpu.VMEM((block, width), jnp.float32),) * 2,
         in_specs=[pl.BlockSpec(memory_space=pltpu.HBM)] * 6,
@@ -265,6 +277,14 @@
         ],
         compiler_params=pltpu.CompilerParams(collective_id=0, has_side_effects=True),
     )(acts, cot, params, first, second, outer)
+    return pl.pallas_call(
+        write_out,
+        out_shape=(jax.ShapeDtypeStruct((block, width), jnp.float32),) * 2,
+        in_specs=[pl.BlockSpec(memory_space=pltpu.VMEM)] * 2,
+        out_specs=(pl.BlockSpec(memory_space=pltpu.HBM),) * 2,
+        scratch_shapes=[pltpu.SemaphoreType.DMA((2, PIECES))],
+        compiler_params=pltpu.CompilerParams(vmem_limit_bytes=16 * block * width),
+    )(*results)
 
 def plain_sum(acts, cot, first, second):
     inputs = lax.all_to_all(acts, "fsdp", split_axis=1, concat_axis=0, tiled=True)

time: 37.2 us -> 36.6 us (0.984)
  local copies, waits for them, and re-layouts: 1.59 us -> 0 us
  Pallas kernels: 34.8 us -> 35.8 us
    unnamed x2 -> x0, local copies, waits for them, and re-layouts: 1.59 us -> none
    pallas_call x0 -> x1, Pallas kernels: none -> 1 us  [fused_round(): pl.pallas_call(write_out, out_shape=(jax.ShapeDtypeStruct((block, width),...]
where the time goes in v2:
time: 36.6 us; the launch traced here: 36.4 us
  Pallas kernels  35.8 us (98%)
  between operations  0.64 us (2%)
    pallas_call x1, Pallas kernels, fused_round(): pl.pallas_call(functools.partial(kernel, n_rep), out_shape=(pltpu.VMEM((b...  34.8 us
    pallas_call x1, Pallas kernels, fused_round(): pl.pallas_call(write_out, out_shape=(jax.ShapeDtypeStruct((block, width),...  1 us

profile of v2, /device:TPU:0, one launch (start us, length us, event | category | flops | bytes accessed | tf_op | source)
XLA Modules:
  0.0 36.4 jit_solution(361250385334124743)
XLA Ops:
  0.6 34.8 %shard_map.77 = (f32[256,512]{1,0:T(8,128)S(1)}, f32[256,512]{1,0:T(8,128)S(1)}) custom-call(bf16[128,8192]{1,0:T(8,128)(2,1)} %bitcast.2, bf16[128,512]{1,0:T(8,128)(2,1)} %bitcast.3, f32[2048,512]{1,0:T(8,128)} %params_ref.1, f32[2048,512]{1,0:T(8,128)} %first_ref.1, f32[2048,512]{1,0:T(8,128)} %second_ref.1, f32[256,512]{1,0:T(8,128)} %outer_ref.1), custom_call_target="tpu_custom_call" | custom-call | tf_op jit(solution)/shard_map/pallas_call | solution.py:254
  35.4 1.0 %shard_map.78 = (f32[256,512]{1,0:T(8,128)}, f32[256,512]{1,0:T(8,128)}) custom-call(f32[256,512]{1,0:T(8,128)S(1)} %get-tuple-element.4.params_ref, f32[256,512]{1,0:T(8,128)S(1)} %get-tuple-element.5.mom_ref), custom_call_target="tpu_custom_call" | custom-call | tf_op jit(solution)/shard_map/pallas_call | solution.py:280

commit v3 on v2

--- a/solution.py
+++ b/solution.py
@@ -25,9 +25,9 @@
     (2, 1, 2, 1, (3, 1)), (3, 1, 3, 1, (2, 1)), (0, 0, None, None, None), (0, 1, None, None, None),
 )
 UNIT = 128
-WINDOW = 5
+WINDOW = 6
 EARLY = 1
-PIECES = 2
+PIECES = 1
 AFTER = 4
 
 def adamw_direction(first, second, gradient):
@@ -96,23 +96,21 @@
         pltpu.make_async_copy(params_ref.at[span(rep * block, block)], anchor_buf, local_sem.at[4]),
         pltpu.make_async_copy(outer_ref, outer_buf, local_sem.at[5]),
     ]
-    for copy in local[:2]:
+    for copy in local + finals:
         copy.start()
     pl.semaphore_wait(barrier, len(peers) + 1 - outer)
 
+    local[0].wait()
     pieces = (pl.ds(0, half), pl.ds(half, half))
     direct = {}
     for turn in range(2):
         for d in (1, 2):
             piece = (d - 1 + turn) % 2
             direct[d, piece] = remote(
-                cot_ref.at[pieces[piece]], cot_buf.at[d, pieces[piece]],
+                cot_buf.at[0, pieces[piece]], cot_buf.at[d, pieces[piece]],
                 send_sem.at[0], cot_recv.at[d - 1, piece], (rep, shards[d]),
             )
             direct[d, piece].start()
-
-    for copy in local[2:] + finals:
-        copy.start()
 
     def issue(i):
         at = units[i][2]
@@ -136,7 +134,7 @@
         relays.append(relay)
     for i in range(EARLY, AFTER):
         issue(i)
-    for copy in local:
+    for copy in local[1:]:
         copy.wait()
     for d in (1, 2):
         direct[d, 2 - d].wait_recv()

time: 36.6 us -> 36.4 us (level)
  no operation moved by 1% of the time
where the time goes in v3:
time: 36.4 us; the launch traced here: 36.3 us
  Pallas kernels  35.6 us (98%)
  between operations  0.64 us (2%)
    pallas_call x1, Pallas kernels, fused_round(): pl.pallas_call(functools.partial(kernel, n_rep), out_shape=(pltpu.VMEM((b...  34.6 us
    pallas_call x1, Pallas kernels, fused_round(): pl.pallas_call(write_out, out_shape=(jax.ShapeDtypeStruct((block, width),...  0.99 us

profile of v3, /device:TPU:0, one launch (start us, length us, event | category | flops | bytes accessed | tf_op | source)
XLA Modules:
  0.0 36.3 jit_solution(4125031784464884887)
XLA Ops:
  0.6 34.6 %shard_map.77 = (f32[256,512]{1,0:T(8,128)S(1)}, f32[256,512]{1,0:T(8,128)S(1)}) custom-call(bf16[128,8192]{1,0:T(8,128)(2,1)} %bitcast.2, bf16[128,512]{1,0:T(8,128)(2,1)} %bitcast.3, f32[2048,512]{1,0:T(8,128)} %params_ref.1, f32[2048,512]{1,0:T(8,128)} %first_ref.1, f32[2048,512]{1,0:T(8,128)} %second_ref.1, f32[256,512]{1,0:T(8,128)} %outer_ref.1), custom_call_target="tpu_custom_call" | custom-call | tf_op jit(solution)/shard_map/pallas_call | solution.py:252
  35.3 1.0 %shard_map.78 = (f32[256,512]{1,0:T(8,128)}, f32[256,512]{1,0:T(8,128)}) custom-call(f32[256,512]{1,0:T(8,128)S(1)} %get-tuple-element.4.params_ref, f32[256,512]{1,0:T(8,128)S(1)} %get-tuple-element.5.mom_ref), custom_call_target="tpu_custom_call" | custom-call | tf_op jit(solution)/shard_map/pallas_call | solution.py:278

commit v4 on v3

--- a/solution.py
+++ b/solution.py
@@ -170,8 +170,6 @@
         rows_at = span(at, size)
         arrived = acts_buf.at[1:, :, rows_at]
         remote(arrived, arrived, send_sem.at[1], acts_recv.at[i], (rep, shards[1])).wait_recv()
-        if h == 0 and i + WINDOW < len(units):
-            issue(i + WINDOW)
         gradient = lax.dot_general(
             acts_buf[:, :, rows_at].reshape(tokens, size), cot_buf[...].reshape(tokens, width),
             (((0,), (0,)), ((), ())), preferred_element_type=jnp.float32,
@@ -185,6 +183,8 @@
             pairing.start()
             while held:
                 combine(held.pop())
+            if i + WINDOW < len(units):
+                issue(i + WINDOW)
             continue
         pairing.wait_recv()
         value = value + pair_in[step]

time: 36.4 us -> 36.4 us (level)
  no operation moved by 1% of the time
where the time goes in v4:
time: 36.4 us; the launch traced here: 36.3 us
  Pallas kernels  35.6 us (98%)
  between operations  0.64 us (2%)
    pallas_call x1, Pallas kernels, fused_round(): pl.pallas_call(functools.partial(kernel, n_rep), out_shape=(pltpu.VMEM((b...  34.6 us
    pallas_call x1, Pallas kernels, fused_round(): pl.pallas_call(write_out, out_shape=(jax.ShapeDtypeStruct((block, width),...  0.99 us

profile of v4, /device:TPU:0, one launch (start us, length us, event | category | flops | bytes accessed | tf_op | source)
XLA Modules:
  0.0 36.3 jit_solution(5138065546543756388)
XLA Ops:
  0.6 34.6 %shard_map.77 = (f32[256,512]{1,0:T(8,128)S(1)}, f32[256,512]{1,0:T(8,128)S(1)}) custom-call(bf16[128,8192]{1,0:T(8,128)(2,1)} %bitcast.2, bf16[128,512]{1,0:T(8,128)(2,1)} %bitcast.3, f32[2048,512]{1,0:T(8,128)} %params_ref.1, f32[2048,512]{1,0:T(8,128)} %first_ref.1, f32[2048,512]{1,0:T(8,128)} %second_ref.1, f32[256,512]{1,0:T(8,128)} %outer_ref.1), custom_call_target="tpu_custom_call" | custom-call | tf_op jit(solution)/shard_map/pallas_call | solution.py:252
  35.3 1.0 %shard_map.78 = (f32[256,512]{1,0:T(8,128)}, f32[256,512]{1,0:T(8,128)}) custom-call(f32[256,512]{1,0:T(8,128)S(1)} %get-tuple-element.4.params_ref, f32[256,512]{1,0:T(8,128)S(1)} %get-tuple-element.5.mom_ref), custom_call_target="tpu_custom_call" | custom-call | tf_op jit(solution)/shard_map/pallas_call | solution.py:278
